TPU v7x, 32 devices: a whole 2x2x4 slice. The times are simulated.
32 devices in a mesh: cuts: 4 (over z), row: 8 (over y, x, core).
Axes of the slice: x: 2, y: 2, z: 4, core: 2. Of those that a mesh axis runs over, the one named last changes fastest.
Arguments:
- eigvecs: float32 [16384, 2048], P('row', 'cuts'), may hold values from -1.2 to 1.2
- slice_counts: int32 [4], P('cuts'), may hold values from 256 to 512, as said below
- occ_index: int32 [2048], P('cuts'), may hold values from 0 to 63
- occ_levels: float32 [64], replicated, may hold values from 0 to 1
Outputs:
- slab: float32 [4096, 16384], P('cuts', 'row')
Inputs may be any that keep to these rules, and one draw needn't show every extreme that they name: `slice_counts`: some slice holds exactly 512 eigenvalues in every draw; the others at least half of that.
All inputs are finite; a program needn't handle non-finite values.
Results may differ from a plain program's by a relative error of at most 0.000062.
Values sent between devices are 32-bit elements; how exact they have to be, the bound alone decides.
No kernel may reach another device: no remote copies, remote signals or barrier semaphores. Data moves between devices by JAX's collectives and lax.ppermute only.
A program may use at most 128 MiB of HBM per device.

v0:
```python
import jax
import jax.numpy as jnp
from jax import lax
from jax.sharding import PartitionSpec as P

BLOCK = 1024
SLAB_SUB = 256
SLAB = 4096


def shards(eigvecs, slice_counts, occ_index, occ_levels):
    row_count = eigvecs.shape[0]
    slot_count = eigvecs.shape[1]
    level_ids = jnp.arange(occ_levels.shape[0], dtype=jnp.int32)
    one_hot = (occ_index[:, None] == level_ids[None, :]).astype(jnp.float32)
    values = jnp.dot(one_hot, occ_levels, precision=lax.Precision.HIGHEST)
    live = jnp.arange(slot_count, dtype=jnp.int32) < slice_counts[0]
    weights = jnp.where(live, values, jnp.float32(0.0))
    local_blocks = eigvecs.reshape(row_count // BLOCK, BLOCK, slot_count)[:, :SLAB_SUB, :]
    local_rows = local_blocks.reshape(-1, slot_count) * weights[None, :]
    cut_count = lax.axis_size("cuts")
    row_devices = lax.axis_size("row")
    owned = SLAB // cut_count
    strip = slot_count // row_devices
    spread = lax.all_to_all(local_rows.T, "row", split_axis=0, concat_axis=1, tiled=True)
    owners = lax.all_to_all(spread, "cuts", split_axis=1, concat_axis=0, tiled=True)
    panels = lax.all_gather(owners, "row", axis=0, tiled=True)
    panel = (
        panels.reshape(row_devices, cut_count, strip, owned)
        .transpose(1, 0, 2, 3)
        .reshape(cut_count * slot_count, owned)
    )
    return lax.dot_general(
        panel,
        lax.all_gather(eigvecs, "cuts", axis=1, tiled=True),
        (((0,), (1,)), ((), ())),
        precision=lax.Precision.HIGHEST,
        preferred_element_type=jnp.float32,
    )


def solution(mesh):
    return jax.shard_map(
        shards,
        mesh=mesh,
        in_specs=(P("row", "cuts"), P("cuts"), P("cuts"), P()),
        out_specs=P("cuts", "row"),
        check_vma=False,
    )
```

profile of v0, /device:TPU:0, one launch (start us, length us, event | category | flops | bytes accessed | tf_op | source)
XLA Modules:
  0.0 519.5 jit_solution(15764011367793498607)
XLA Ops:
  6.5 0.0 copy-start
  6.5 0.0 all-gather.3.cloned.1.call-start
  7.2 1.3 slice.4
  8.5 0.3 copy.14
  8.8 0.0 copy-done
  8.9 1.0 fusion
  9.9 0.2 broadcast_multiply_fusion
  10.0 20.3 %all_to_all.35 = f32[8,64,512]{2,1,0:T(8,128)S(1)} all-to-all(f32[8,64,512]{2,1,0:T(8,128)S(1)} %bitcast.24), channel_id=1, replica_groups=mesh['cuts'=4,'row'=8] {'row'}, dimensions={0} | all-to-all | bytes 2097152 | tf_op jit(solution)/shard_map/all_to_all | solution.py:25
  30.3 0.6 copy.10
  31.0 0.5 all_to_all.29
  31.5 0.6 copy.11
  32.1 29.9 %all_to_all.36 = f32[64,4,1024]{2,0,1:T(8,128)} all-to-all(f32[64,4,1024]{2,0,1:T(8,128)S(1)} %copy.11), channel_id=1, replica_groups=mesh['cuts'=4,'row'=8] {'cuts'}, dimensions={1} | all-to-all | bytes 2097152 | tf_op jit(solution)/shard_map/all_to_all | solution.py:26
  62.0 0.0 all-gather.3.cloned.1.call-update
  62.1 0.0 all-gather.5.cloned.1.call-start
  62.1 0.7 all-gather.5.cloned.1.call-update
  62.8 51.5 %all-gather.3.cloned.1.call-done = f32[2048,1024]{1,0:T(8,128)} async-done(((f32[256,1024]{1,0:T(8,128)}), f32[2048,1024]{1,0:T(8,128)}) %all-gather.3.cloned.1.call-update) | async-done | bytes 8388624 | tf_op jit(solution)/shard_map/all_gather | solution.py:27
  114.3 8.3 %copy.12 = f32[8,4,64,1024]{3,2,0,1:T(8,128)} copy(f32[8,4,64,1024]{3,2,1,0:T(8,128)} %bitcast.21) | data formatting | bytes 16777216 | tf_op jit(solution)/shard_map/reshape | solution.py:29
  122.6 280.1 %all-gather.5.cloned.1.call-done = f32[2048,2048]{1,0:T(8,128)} async-done(((f32[2048,512]{1,0:T(8,128)}), f32[2048,2048]{1,0:T(8,128)}) %all-gather.5.cloned.1.call-update) | async-done | bytes 16777232 | tf_op jit(solution)/shard_map/all_gather | solution.py:35
  402.7 110.0 %fusion.4 = f32[1024,2048]{1,0:T(8,128)} fusion(f32[2048,1024]{1,0:T(8,128)} %bitcast.22, f32[2048,2048]{1,0:T(8,128)} %all-gather.5.cloned.1.call-done), kind=kOutput, calls=%fused_computation.7 | convolution fusion | flops 51539607552 | bytes 33554432 | tf_op jit(solution)/shard_map/dot_general | solution.py:33
  (1 shorter events, 0.0 us)
Async XLA Ops:
  6.5 2.3 copy-start
  6.5 107.8 %all-gather.3.cloned.1.call-start = ((), (), s32[]{:S(2)}) async-start(), calls=%async_computation.2 | async-start | bytes 9437184 | tf_op jit(solution)/shard_map/all_gather | solution.py:27
  62.1 340.6 %all-gather.5.cloned.1.call-start = ((), (), s32[]{:S(2)}) async-start(), calls=%async_computation.3 | async-start | bytes 20971520 | tf_op jit(solution)/shard_map/all_gather | solution.py:35
Sparse Core Ops, SparseCore 0:
  62.2 52.0 all-gather.2
  115.9 286.7 all-gather.4
where the time goes:
time: 520 us; the launch traced here: 519 us
  waiting for transfers between devices  332 us (64%)
  matrix products  111 us (21%)
  blocking collectives  50.3 us (10%)
  between operations  14.1 us (3%)
  local copies, waits for them, and re-layouts  11.6 us (2%)
    all_gather x1, waiting for transfers between devices, shards(): lax.all_gather(eigvecs, 'cuts', axis=1, tiled=True)  280 us
    dot_general x1, matrix products, shards(): lax.dot_general(panel, lax.all_gather(eigvecs, 'cuts', axis=1, tiled=True...  110 us
    all_gather x1, waiting for transfers between devices, shards(): panels = lax.all_gather(owners, 'row', axis=0, tiled=True)  51.5 us
    all_to_all x1, blocking collectives, shards(): lax.all_to_all(spread, 'cuts', split_axis=1, concat_axis=0, tiled=True)  29.9 us
    all_to_all x1, blocking collectives, shards(): lax.all_to_all(local_rows.T, 'row', split_axis=0, concat_axis=1, tiled=True)  20.3 us
  transfers between devices with their start and end apart: 2, of which 2 were waited for; matrix products, arithmetic and copies ran while one was open for 2% of the time, Pallas kernels for 0%

commit v1 on v0

--- a/solution.py
+++ b/solution.py
@@ -6,6 +6,17 @@
 BLOCK = 1024
 SLAB_SUB = 256
 SLAB = 4096
+
+
+def gather_by_hops(x, mesh_axis, along):
+    size = lax.axis_size(mesh_axis)
+    right = [(i, (i + 1) % size) for i in range(size)]
+    parts = [x]
+    for hop in range(1, size):
+        parts = [lax.ppermute(parts[0], mesh_axis, right), *parts]
+    out = jnp.concatenate(parts, axis=along)
+    places = (lax.axis_index(mesh_axis) + 1) * parts[-1].shape[along]
+    return jnp.roll(out, places, axis=along)
 
 
 def shards(eigvecs, slice_counts, occ_index, occ_levels):
@@ -24,7 +35,7 @@
     strip = slot_count // row_devices
     spread = lax.all_to_all(local_rows.T, "row", split_axis=0, concat_axis=1, tiled=True)
     owners = lax.all_to_all(spread, "cuts", split_axis=1, concat_axis=0, tiled=True)
-    panels = lax.all_gather(owners, "row", axis=0, tiled=True)
+    panels = gather_by_hops(owners, "row", 0)
     panel = (
         panels.reshape(row_devices, cut_count, strip, owned)
         .transpose(1, 0, 2, 3)

time: 520 us -> 438 us (0.84)
  waiting for transfers between devices: 332 us -> 197 us
  local copies, waits for them, and re-layouts: 11.6 us -> 41.1 us
  blocking collectives: 50.3 us -> 73.8 us
    all_gather x1, waiting for transfers between devices: 280 us -> 90.4 us  [shards(): lax.all_gather(eigvecs, 'cuts', axis=1, tiled=True)]
    ppermute x0 -> x7, waiting for transfers between devices: none -> 106 us  [gather_by_hops(): parts = [lax.ppermute(parts[0], mesh_axis, right), *parts]]
    all_gather x1 -> x0, waiting for transfers between devices: 51.5 us -> none  [shards(): panels = lax.all_gather(owners, 'row', axis=0, tiled=True)]
    unnamed x2 -> x31, local copies, waits for them, and re-layouts: 0.01 us -> 28.2 us
    all_to_all x1, blocking collectives: 29.9 us -> 53.5 us  [shards(): lax.all_to_all(spread, 'cuts', split_axis=1, concat_axis=0, tiled=True)]
    reshape x1 -> x0, local copies, waits for them, and re-layouts: 8.28 us -> none  [shards(): panels.reshape(row_devices, cut_count, strip, owned).transpose(1, 0, 2, 3)]
  transfers between devices with their start and end apart: 2 -> 8, of which waited for: 2 -> 8; matrix products, arithmetic and copies ran while one was open for 2% -> 9% of each run, Pallas kernels for 0% -> 0%
where the time goes in v1:
time: 438 us
  waiting for transfers between devices  197 us (45%)
  matrix products  111 us (25%)
  blocking collectives  73.8 us (17%)
  local copies, waits for them, and re-layouts  41.1 us (9%)
  between operations  14.1 us (3%)
    dot_general x1, matrix products, shards(): lax.dot_general(panel, lax.all_gather(eigvecs, 'cuts', axis=1, tiled=True...  110 us
    ppermute x7, waiting for transfers between devices, gather_by_hops(): parts = [lax.ppermute(parts[0], mesh_axis, right), *parts]  106 us
    all_gather x1, waiting for transfers between devices, shards(): lax.all_gather(eigvecs, 'cuts', axis=1, tiled=True)  90.4 us
    all_to_all x1, blocking collectives, shards(): lax.all_to_all(spread, 'cuts', split_axis=1, concat_axis=0, tiled=True)  53.5 us
    unnamed x31, local copies, waits for them, and re-layouts  28.2 us
    all_to_all x1, blocking collectives, shards(): lax.all_to_all(local_rows.T, 'row', split_axis=0, concat_axis=1, tiled=True)  20.3 us
  transfers between devices with their start and end apart: 8, of which 8 were waited for; matrix products, arithmetic and copies ran while one was open for 9% of the time, Pallas kernels for 0%

profile of v1, /device:TPU:0, one launch (start us, length us, event | category | flops | bytes accessed | tf_op | source)
XLA Modules:
  0.0 437.6 jit_solution(12167061029819645873)
XLA Ops:
  7.3 1.3 slice.4
  9.6 1.0 fusion
  10.7 20.3 %all_to_all.35 = f32[8,64,512]{2,1,0:T(8,128)S(1)} all-to-all(f32[8,64,512]{2,1,0:T(8,128)S(1)} %bitcast.27), channel_id=1, replica_groups=mesh['cuts'=4,'row'=8] {'row'}, dimensions={0} | all-to-all | bytes 2097152 | tf_op jit(solution)/shard_map/all_to_all | solution.py:36
  32.8 53.5 %all_to_all.36 = f32[64,4,1024]{2,0,1:T(8,128)S(1)} all-to-all(f32[64,4,1024]{2,0,1:T(8,128)S(1)} %copy.14), channel_id=1, replica_groups=mesh['cuts'=4,'row'=8] {'cuts'}, dimensions={1} | all-to-all | bytes 2097152 | tf_op jit(solution)/shard_map/all_to_all | solution.py:37
  86.3 15.1 %collective-permute-done = f32[256,1024]{1,0:T(8,128)S(1)} collective-permute-done((f32[256,1024]{1,0:T(8,128)S(1)}, f32[256,1024]{1,0:T(8,128)S(1)}, u32[]{:S(2)}, u32[]{:S(2)}) %collective-permute-start) | collective-permute-done | bytes 1048608 | tf_op jit(solution)/shard_map/ppermute | solution.py:16
  101.4 15.1 %collective-permute-done.1 = f32[256,1024]{1,0:T(8,128)S(1)} collective-permute-done((f32[256,1024]{1,0:T(8,128)S(1)}, f32[256,1024]{1,0:T(8,128)S(1)}, u32[]{:S(2)}, u32[]{:S(2)}) %collective-permute-start.1) | collective-permute-done | bytes 1048608 | tf_op jit(solution)/shard_map/ppermute | solution.py:16
  116.6 15.1 %collective-permute-done.2 = f32[256,1024]{1,0:T(8,128)S(1)} collective-permute-done((f32[256,1024]{1,0:T(8,128)S(1)}, f32[256,1024]{1,0:T(8,128)S(1)}, u32[]{:S(2)}, u32[]{:S(2)}) %collective-permute-start.2) | collective-permute-done | bytes 1048608 | tf_op jit(solution)/shard_map/ppermute | solution.py:16
  131.7 1.0 copy-done.2
  132.7 15.1 %collective-permute-done.3 = f32[256,1024]{1,0:T(8,128)S(1)} collective-permute-done((f32[256,1024]{1,0:T(8,128)S(1)}, f32[256,1024]{1,0:T(8,128)S(1)}, u32[]{:S(2)}, u32[]{:S(2)}) %collective-permute-start.3) | collective-permute-done | bytes 1048608 | tf_op jit(solution)/shard_map/ppermute | solution.py:16
  148.8 15.1 %collective-permute-done.4 = f32[256,1024]{1,0:T(8,128)S(1)} collective-permute-done((f32[256,1024]{1,0:T(8,128)S(1)}, f32[256,1024]{1,0:T(8,128)S(1)}, u32[]{:S(2)}, u32[]{:S(2)}) %collective-permute-start.4) | collective-permute-done | bytes 1048608 | tf_op jit(solution)/shard_map/ppermute | solution.py:16
  164.9 15.2 %collective-permute-done.5 = f32[256,1024]{1,0:T(8,128)} collective-permute-done((f32[256,1024]{1,0:T(8,128)S(1)}, f32[256,1024]{1,0:T(8,128)}, u32[]{:S(2)}, u32[]{:S(2)}) %collective-permute-start.5) | collective-permute-done | bytes 1048608 | tf_op jit(solution)/shard_map/ppermute | solution.py:16
  180.1 15.4 %collective-permute-done.6 = f32[256,1024]{1,0:T(8,128)} collective-permute-done((f32[256,1024]{1,0:T(8,128)}, f32[256,1024]{1,0:T(8,128)}, u32[]{:S(2)}, u32[]{:S(2)}) %collective-permute-start.6) | collective-permute-done | bytes 1048608 | tf_op jit(solution)/shard_map/ppermute | solution.py:16
  195.5 2.3 constant_dynamic-update-slice_fusion.15
  197.9 2.4 constant_dynamic-update-slice_fusion.14
  200.2 2.3 constant_dynamic-update-slice_fusion.13
  202.5 2.4 constant_dynamic-update-slice_fusion.12
  204.9 2.3 constant_dynamic-update-slice_fusion.11
  207.2 1.1 constant_dynamic-update-slice_fusion.10
  208.3 1.1 constant_dynamic-update-slice_fusion.9
  209.4 1.2 constant_dynamic-update-slice_fusion.8
  210.6 2.4 constant_dynamic-update-slice_fusion.7
  213.0 2.3 constant_dynamic-update-slice_fusion.6
  215.3 1.1 constant_dynamic-update-slice_fusion.5
  216.4 1.1 constant_dynamic-update-slice_fusion.4
  217.5 1.2 constant_dynamic-update-slice_fusion.3
  218.7 1.0 constant_dynamic-update-slice_fusion.2
  219.7 1.1 constant_dynamic-update-slice_fusion.1
  220.8 1.1 constant_dynamic-update-slice_fusion
  221.9 4.4 %constant_dynamic-slice_fusion = f32[2048,1024]{1,0:T(8,128)S(1)} fusion(f32[4096,1024]{1,0:T(8,128)} %constant_dynamic-update-slice_fusion, s32[]{:T(128)S(6)} %select_n.19), kind=kLoop, calls=%fused_computation.23 | loop fusion | bytes 16777220 | tf_op jit(solution)/shard_map/jit(_roll_dynamic)/dynamic_slice | solution.py:19
  226.3 4.1 copy.15
  230.4 90.4 %all-gather.2.cloned.1.call-done = f32[2048,2048]{1,0:T(8,128)} async-done(((f32[2048,512]{1,0:T(8,128)}), f32[2048,2048]{1,0:T(8,128)}) %all-gather.2.cloned.1.call-update) | async-done | bytes 16777232 | tf_op jit(solution)/shard_map/all_gather | solution.py:46
  320.8 110.0 %fusion.4 = f32[1024,2048]{1,0:T(8,128)} fusion(f32[2048,1024]{1,0:T(8,128)} %bitcast.25, f32[2048,2048]{1,0:T(8,128)} %all-gather.2.cloned.1.call-done), kind=kOutput, calls=%fused_computation.24 | convolution fusion | flops 51539607552 | bytes 33554432 | tf_op jit(solution)/shard_map/dot_general | solution.py:44
  (30 shorter events, 4.9 us)
Async XLA Ops:
  6.5 3.0 copy-start
  6.5 314.3 %all-gather.2.cloned.1.call-start = ((), (), s32[]{:S(2)}) async-start(), calls=%async_computation.2 | async-start | bytes 20971520 | tf_op jit(solution)/shard_map/all_gather | solution.py:46
  86.3 15.1 %collective-permute-start = (f32[256,1024]{1,0:T(8,128)S(1)}, f32[256,1024]{1,0:T(8,128)S(1)}, u32[]{:S(2)}, u32[]{:S(2)}) collective-permute-start(f32[256,1024]{1,0:T(8,128)S(1)} %bitcast.22), channel_id=1, source_target_pairs={{0,1},{1,2},{2,3},{3,4},{4,5},{5,6},{6,7},{7,0},{8,9},{9,10},{10,1... | collective-permute-start | bytes 3145736 | tf_op jit(solution)/shard_map/ppermute | solution.py:16
  101.4 15.1 %collective-permute-start.1 = (f32[256,1024]{1,0:T(8,128)S(1)}, f32[256,1024]{1,0:T(8,128)S(1)}, u32[]{:S(2)}, u32[]{:S(2)}) collective-permute-start(f32[256,1024]{1,0:T(8,128)S(1)} %collective-permute-done), channel_id=1, source_target_pairs={{0,1},{1,2},{2,3},{3,4},{4,5},{5,6},{6,7},{7,0},{8,9},{9,10},{10,1... | collective-permute-start | bytes 3145736 | tf_op jit(solution)/shard_map/ppermute | solution.py:16
  116.6 15.1 %collective-permute-start.2 = (f32[256,1024]{1,0:T(8,128)S(1)}, f32[256,1024]{1,0:T(8,128)S(1)}, u32[]{:S(2)}, u32[]{:S(2)}) collective-permute-start(f32[256,1024]{1,0:T(8,128)S(1)} %collective-permute-done.1), channel_id=1, source_target_pairs={{0,1},{1,2},{2,3},{3,4},{4,5},{5,6},{6,7},{7,0},{8,9},{9,10},{10,1... | collective-permute-start | bytes 3145736 | tf_op jit(solution)/shard_map/ppermute | solution.py:16
  131.7 1.0 copy-start.2
  132.7 15.1 %collective-permute-start.3 = (f32[256,1024]{1,0:T(8,128)S(1)}, f32[256,1024]{1,0:T(8,128)S(1)}, u32[]{:S(2)}, u32[]{:S(2)}) collective-permute-start(f32[256,1024]{1,0:T(8,128)S(1)} %collective-permute-done.2), channel_id=1, source_target_pairs={{0,1},{1,2},{2,3},{3,4},{4,5},{5,6},{6,7},{7,0},{8,9},{9,10},{10,1... | collective-permute-start | bytes 3145736 | tf_op jit(solution)/shard_map/ppermute | solution.py:16
  147.8 1.0 copy-start.4
  148.8 15.1 %collective-permute-start.4 = (f32[256,1024]{1,0:T(8,128)S(1)}, f32[256,1024]{1,0:T(8,128)S(1)}, u32[]{:S(2)}, u32[]{:S(2)}) collective-permute-start(f32[256,1024]{1,0:T(8,128)S(1)} %collective-permute-done.3), channel_id=1, source_target_pairs={{0,1},{1,2},{2,3},{3,4},{4,5},{5,6},{6,7},{7,0},{8,9},{9,10},{10,1... | collective-permute-start | bytes 3145736 | tf_op jit(solution)/shard_map/ppermute | solution.py:16
  163.9 1.0 copy-start.6
  164.9 15.2 %collective-permute-start.5 = (f32[256,1024]{1,0:T(8,128)S(1)}, f32[256,1024]{1,0:T(8,128)}, u32[]{:S(2)}, u32[]{:S(2)}) collective-permute-start(f32[256,1024]{1,0:T(8,128)S(1)} %collective-permute-done.4), channel_id=1, source_target_pairs={{0,1},{1,2},{2,3},{3,4},{4,5},{5,6},{6,7},{7,0},{8,9},{9,10},{10,1... | collective-permute-start | bytes 3145736 | tf_op jit(solution)/shard_map/ppermute | solution.py:16
  180.1 15.4 %collective-permute-start.6 = (f32[256,1024]{1,0:T(8,128)}, f32[256,1024]{1,0:T(8,128)}, u32[]{:S(2)}, u32[]{:S(2)}) collective-permute-start(f32[256,1024]{1,0:T(8,128)} %collective-permute-done.5), channel_id=1, source_target_pairs={{0,1},{1,2},{2,3},{3,4},{4,5},{5,6},{6,7},{7,0},{8,9},{9,10},{10,1... | collective-permute-start | bytes 3145736 | tf_op jit(solution)/shard_map/ppermute | solution.py:16
  180.1 35.2 %copy-start.7 = (f32[256,1024]{1,0:T(8,128)S(1)}, f32[256,1024]{1,0:T(8,128)}, u32[]{:S(2)}) copy-start(f32[256,1024]{1,0:T(8,128)} %copy-done.6) | copy-start | bytes 3145732
  180.1 36.3 %copy-start.5 = (f32[256,1024]{1,0:T(8,128)S(1)}, f32[256,1024]{1,0:T(8,128)}, u32[]{:S(2)}) copy-start(f32[256,1024]{1,0:T(8,128)} %copy-done.4) | copy-start | bytes 3145732
  180.1 37.4 %copy-start.3 = (f32[256,1024]{1,0:T(8,128)S(1)}, f32[256,1024]{1,0:T(8,128)}, u32[]{:S(2)}) copy-start(f32[256,1024]{1,0:T(8,128)} %copy-done.2) | copy-start | bytes 3145732
  320.8 110.0 %copy-start.1 = (f32[64]{0:T(128)S(1)}, f32[64]{0:T(128)}, u32[]{:S(2)}) copy-start(f32[64]{0:T(128)} %param.7) | copy-start | bytes 772
Sparse Core Ops, SparseCore 0:
  8.9 311.8 all-gather.1
